TPU v7x, 32 devices: a whole 2x2x4 slice. The times are simulated.
32 devices in a mesh: expert: 2 (over y), tensor: 16 (over z, x, core).
Axes of the slice: x: 2, y: 2, z: 4, core: 2. Of those that a mesh axis runs over, the one named last changes fastest.
Arguments:
- tokens: bfloat16 [256, 6144], P(('expert', 'tensor')), may hold values from -6 to 6
- expert_ids: int32 [256, 2], P(('expert', 'tensor')), may hold values from 0 to 7, all different within a row; in each aligned block of 8 rows (0 to 7, 8 to 15, ...) at most 3 rows name the same one
- gates: float32 [256, 2], P(('expert', 'tensor')), may hold values from 0.2 to 1
- w_gate: bfloat16 [8, 6144, 8192], P('expert', None, 'tensor'), may hold values from -0.078125 to 0.078125
- w_up: bfloat16 [8, 6144, 8192], P('expert', None, 'tensor'), may hold values from -0.078125 to 0.078125
- w_down: bfloat16 [8, 8192, 6144], P('expert', 'tensor'), may hold values from -0.0625 to 0.0625
Outputs:
- mixed: bfloat16 [256, 6144], P(('expert', 'tensor'))
Inputs may be any that keep to these rules, and one draw needn't show every extreme that they name: `expert_ids`: each token names 2 different experts. Among the tokens of one device (aligned blocks of 8 rows) no expert is named more than 3 times, a bound that some expert reaches in every block.
All inputs are finite; a program needn't handle non-finite values.
Results may differ from a plain program's by a relative error of at most 0.02.
Values may be sent and summed in bfloat16 or wider, within the bound.
A program may use at most 128 MiB of HBM per device.

v0:
```python
import jax
import jax.numpy as jnp
from jax import lax
from jax.sharding import PartitionSpec as P

EXPERTS = 8
TOPK = 2
CAP = 3


def route_places(ids):
    flat = ids.reshape(-1)
    onehot = (flat[:, None] == jnp.arange(EXPERTS, dtype=jnp.int32)[None, :]).astype(jnp.int32)
    before = jnp.cumsum(onehot, axis=0) - onehot
    slot = jnp.sum(before * onehot, axis=1)
    return flat * CAP + slot


def body(tokens, expert_ids, gates, w_gate, w_up, w_down):
    n_groups = lax.axis_size("expert")
    local_experts = w_gate.shape[0]
    width = tokens.shape[1]
    tok_count = tokens.shape[0]
    places = route_places(expert_ids)
    picker = (jnp.arange(EXPERTS * CAP, dtype=jnp.int32)[:, None] == places[None, :]).astype(
        jnp.bfloat16
    )
    doubled = jnp.repeat(tokens, TOPK, axis=0)
    buffer = jnp.dot(picker, doubled, preferred_element_type=jnp.float32).astype(jnp.bfloat16)
    buffer = buffer.reshape(n_groups, local_experts * CAP, width)
    arrived = lax.all_to_all(buffer, "expert", split_axis=0, concat_axis=0, tiled=True)
    regrouped = arrived.reshape(n_groups, local_experts, CAP, width).transpose(1, 0, 2, 3)
    regrouped = regrouped.reshape(local_experts, n_groups * CAP, width)
    piece = lax.all_gather(regrouped, "tensor", axis=1, tiled=True)
    gate_act = jnp.einsum("erd,edf->erf", piece, w_gate, preferred_element_type=jnp.float32)
    up_act = jnp.einsum("erd,edf->erf", piece, w_up, preferred_element_type=jnp.float32)
    hidden = (jax.nn.silu(gate_act) * up_act).astype(jnp.bfloat16)
    piece = hidden
    term = jnp.einsum("erf,efd->red", piece, w_down, preferred_element_type=jnp.float32)
    summed = lax.psum_scatter(
        term.reshape(n_groups * CAP * lax.axis_size("tensor"), local_experts * width).astype(
            jnp.bfloat16
        ),
        "tensor",
        scatter_dimension=0,
        tiled=True,
    )
    results = summed.reshape(n_groups, CAP, local_experts, width)
    returned = lax.all_to_all(results, "expert", split_axis=0, concat_axis=0, tiled=True)
    results_flat = returned.transpose(0, 2, 1, 3).reshape(EXPERTS * CAP, width)
    weights = (jnp.arange(EXPERTS * CAP, dtype=jnp.int32)[None, :] == places[:, None]).astype(
        jnp.float32
    )
    weights = weights * gates.reshape(-1)[:, None]
    weights = jnp.sum(weights.reshape(tok_count, TOPK, EXPERTS * CAP), axis=1)
    mixed = jnp.dot(weights, results_flat.astype(jnp.float32), precision=lax.Precision.HIGHEST)
    return mixed.astype(jnp.bfloat16)


def solution(mesh):
    return jax.shard_map(
        body,
        mesh=mesh,
        in_specs=(
            P(("expert", "tensor"), None),
            P(("expert", "tensor"), None),
            P(("expert", "tensor"), None),
            P("expert", None, "tensor"),
            P("expert", None, "tensor"),
            P("expert", "tensor", None),
        ),
        out_specs=P(("expert", "tensor"), None),
        check_vma=False,
    )
```

profile of v0, /device:TPU:19, one launch (start us, length us, event | category | flops | bytes accessed | tf_op | source)
XLA Modules:
  0.0 246.6 jit_solution(2106851167836730849)
XLA Ops:
  6.5 0.8 copy.28
  7.3 0.1 eq.43
  7.5 0.2 select_reduce_fusion.1
  7.7 1.0 broadcast_in_dim.2
  8.8 0.2 convolution_convert_fusion.1
  9.1 8.2 %all_to_all.10 = bf16[2,12,6144]{2,1,0:T(8,128)(2,1)S(1)} all-to-all(bf16[2,12,6144]{2,1,0:T(8,128)(2,1)S(1)} %reshape.54), channel_id=1, replica_groups=mesh['expert'=2,'tensor'=16] {'expert'}, dimensions={0} | all-to-all | bytes 589824 | tf_op jit(solution)/shard_map/all_to_all | solution.py:31
  17.3 0.3 copy.31
  17.6 0.9 copy.32
  18.5 53.3 %all-gather.2.cloned.1.call-done = bf16[4,96,6144]{2,0,1:T(4,128)(2,1)} async-done(((bf16[4,6,6144]{2,0,1:T(4,128)(2,1)}), bf16[4,96,6144]{2,0,1:T(4,128)(2,1)}) %all-gather.2.cloned.1.call-update) | async-done | bytes 4718608 | tf_op jit(solution)/shard_map/all_gather | solution.py:34
  71.8 14.0 %fusion.4 = f32[4,96,512]{2,1,0:T(8,128)S(1)} fusion(bf16[4,6144,512]{2,1,0:T(8,128)(2,1)} %param.9, bf16[4,96,6144]{2,0,1:T(4,128)(2,1)} %all-gather.2.cloned.1.call-done), kind=kOutput, calls=%fused_computation.6 | convolution fusion | flops 2415919104 | bytes 30670848 | tf_op jit(solution)/shard_map/erd,edf->erf/dot_general | solution.py:35
  85.9 15.0 %fusion.9 = bf16[4,96,512]{2,1,0:T(8,128)(2,1)S(1)} fusion(bf16[4,6144,512]{2,1,0:T(8,128)(2,1)} %param.10, bf16[4,96,6144]{2,0,1:T(4,128)(2,1)S(1)} %copy-done, f32[4,96,512]{2,1,0:T(8,128)S(1)} %fusion.4), kind=kOutput, calls=%fused_computation.9 | convolution fusion | flops 2417098752 | bytes 31064064 | tf_op jit(solution)/shard_map/erd,edf->erf/dot_general | solution.py:36
  100.8 12.5 %fusion.1 = bf16[4,12,8,6144]{3,2,1,0:T(8,128)(2,1)S(1)} fusion(bf16[4,96,512]{2,1,0:T(8,128)(2,1)S(1)} %fusion.9, bf16[4,512,6144]{2,1,0:T(8,128)(2,1)} %param.11), kind=kOutput, calls=%fused_computation.1 | convolution fusion | flops 2418278400 | bytes 30277632 | tf_op jit(solution)/shard_map/erf,efd->red/dot_general | solution.py:39
  113.3 2.6 %copy.37 = bf16[4,12,8,6144]{3,2,0,1:T(8,128)(2,1)} copy(bf16[4,12,8,6144]{3,2,1,0:T(8,128)(2,1)S(1)} %fusion.1) | data formatting | bytes 9437184 | tf_op jit(solution)/shard_map/convert_element_type | solution.py:41
  116.0 69.9 %fusion = bf16[8,24576]{1,0:T(8,128)(2,1)S(1)} fusion(bf16[96,24576]{1,0:T(8,128)(2,1)} %bitcast.19), kind=kCustom, calls=%all-reduce-scatter | all-reduce-scatter fusion | flops 3145729 | bytes 5112320
  185.8 6.1 %collective-permute-start.2 = (bf16[8,24576]{1,0:T(8,128)(2,1)S(1)}, bf16[8,24576]{1,0:T(8,128)(2,1)S(1)}, u32[]{:S(2)}, u32[]{:S(2)}) collective-permute-start(bf16[8,24576]{1,0:T(8,128)(2,1)S(1)} %fusion), channel_id=1, source_target_pairs={{0,3},{1,4},{2,5},{3,6},{4,7},{5,8},{6,9},{7,10},{8,11},{9,12},{10... | collective-permute-start | bytes 1179656
  192.0 1.9 collective-permute-start.1
  193.9 2.7 %collective-permute-start = (bf16[8,24576]{1,0:T(8,128)(2,1)S(1)}, bf16[8,24576]{1,0:T(8,128)(2,1)S(1)}, u32[]{:S(2)}, u32[]{:S(2)}) collective-permute-start(bf16[8,24576]{1,0:T(8,128)(2,1)S(1)} %fusion), channel_id=1, source_target_pairs={{0,1},{1,2},{2,3},{3,4},{4,5},{5,6},{6,7},{7,8},{8,9},{9,10},{10,1... | collective-permute-start | bytes 1179656
  196.6 0.1 slice
  196.7 1.9 collective-permute-start.3
  198.7 0.1 reduce_sum.21
  198.8 0.6 dynamic-slice.4
  200.0 22.6 %collective-permute-done.3 = bf16[6,24576]{1,0:T(8,128)(2,1)S(1)} collective-permute-done((bf16[6,24576]{1,0:T(8,128)(2,1)S(1)}, bf16[6,24576]{1,0:T(8,128)(2,1)S(1)}, u32[]{:S(2)}, u32[]{:S(2)}) %collective-permute-start.3) | collective-permute-done | bytes 294944
  222.6 0.7 copy-done.1
  223.3 6.1 %concatenate = bf16[38,24576]{1,0:T(8,128)(2,1)S(1)} concatenate(bf16[6,24576]{1,0:T(8,128)(2,1)} %copy-done.1, bf16[8,24576]{1,0:T(8,128)(2,1)S(1)} %collective-permute-done.2, bf16[8,24576]{1,0:T(8,128)(2,1)S(1)} %collective-permute-done.1, bf16[8,24576]{1,0:T(8,128)(2,1)S(1)} %collective-permute-done, bf16[8,24576]{1,0:T(8,128)(2,1)S(1)} %fusion), dimensions={0} | concatenate | bytes 3735552
  229.4 0.1 constant_dynamic-slice_fusion
  229.6 1.1 reshape.57
  230.7 3.4 %all-to-all-start.1 = ((bf16[2,3,4,6144]{3,2,1,0:T(4,128)(2,1)}), bf16[2,3,4,6144]{3,2,1,0:T(4,128)(2,1)S(1)}, u32[]{:S(2)}, u32[]{:S(2)}) async-start(bf16[2,3,4,6144]{3,2,1,0:T(4,128)(2,1)} %reshape.57), calls=%async_computation.1 | async-start | bytes 589824 | tf_op jit(solution)/shard_map/all_to_all | solution.py:49
  234.2 0.1 copy.30
  234.3 4.0 %all-to-all-done.1 = bf16[2,3,4,6144]{3,2,1,0:T(4,128)(2,1)S(1)} async-done(((bf16[2,3,4,6144]{3,2,1,0:T(4,128)(2,1)}), bf16[2,3,4,6144]{3,2,1,0:T(4,128)(2,1)S(1)}, u32[]{:S(2)}, u32[]{:S(2)}) %all-to-all-start.1) | async-done | bytes 294944 | tf_op jit(solution)/shard_map/all_to_all | solution.py:49
  238.3 0.3 copy.36
  238.6 0.3 reshape.58
  238.8 0.9 convolution_convert_fusion.2
  (19 shorter events, 0.4 us)
Async XLA Ops:
  6.5 65.3 %all-gather.2.cloned.1.call-start = ((), (), s32[]{:S(2)}) async-start(), calls=%async_computation.2 | async-start | bytes 5013504 | tf_op jit(solution)/shard_map/all_gather | solution.py:34
  71.8 14.0 %copy-start = (bf16[4,96,6144]{2,0,1:T(4,128)(2,1)S(1)}, bf16[4,96,6144]{2,0,1:T(4,128)(2,1)}, u32[]{:S(2)}) copy-start(bf16[4,96,6144]{2,0,1:T(4,128)(2,1)} %all-gather.2.cloned.1.call-done) | copy-start | bytes 14155780
  113.3 85.4 %copy-start.3 = (u32[32]{0:T(128)S(1)}, u32[32]{0:T(128)}, u32[]{:S(2)}) copy-start(u32[32]{0:T(128)} %constant.19) | copy-start | bytes 388
  116.0 118.3 %copy-start.2 = (f32[8,2]{0,1:T(2,128)S(1)}, f32[8,2]{0,1:T(2,128)}, u32[]{:S(2)}) copy-start(f32[8,2]{0,1:T(2,128)} %param.8) | copy-start | bytes 196
  185.8 36.7 %collective-permute-start.2 = (bf16[8,24576]{1,0:T(8,128)(2,1)S(1)}, bf16[8,24576]{1,0:T(8,128)(2,1)S(1)}, u32[]{:S(2)}, u32[]{:S(2)}) collective-permute-start(bf16[8,24576]{1,0:T(8,128)(2,1)S(1)} %fusion), channel_id=1, source_target_pairs={{0,3},{1,4},{2,5},{3,6},{4,7},{5,8},{6,9},{7,10},{8,11},{9,12},{10... | collective-permute-start | bytes 1179656
  192.0 30.6 %collective-permute-start.1 = (bf16[8,24576]{1,0:T(8,128)(2,1)S(1)}, bf16[8,24576]{1,0:T(8,128)(2,1)S(1)}, u32[]{:S(2)}, u32[]{:S(2)}) collective-permute-start(bf16[8,24576]{1,0:T(8,128)(2,1)S(1)} %fusion), channel_id=1, source_target_pairs={{0,2},{1,3},{2,4},{3,5},{4,6},{5,7},{6,8},{7,9},{8,10},{9,11},{10,... | collective-permute-start | bytes 1179656
  193.9 29.4 %collective-permute-start = (bf16[8,24576]{1,0:T(8,128)(2,1)S(1)}, bf16[8,24576]{1,0:T(8,128)(2,1)S(1)}, u32[]{:S(2)}, u32[]{:S(2)}) collective-permute-start(bf16[8,24576]{1,0:T(8,128)(2,1)S(1)} %fusion), channel_id=1, source_target_pairs={{0,1},{1,2},{2,3},{3,4},{4,5},{5,6},{6,7},{7,8},{8,9},{9,10},{10,1... | collective-permute-start | bytes 1179656
  196.7 25.8 %collective-permute-start.3 = (bf16[6,24576]{1,0:T(8,128)(2,1)S(1)}, bf16[6,24576]{1,0:T(8,128)(2,1)S(1)}, u32[]{:S(2)}, u32[]{:S(2)}) collective-permute-start(bf16[6,24576]{1,0:T(8,128)(2,1)S(1)} %slice), channel_id=1, source_target_pairs={{0,4},{1,5},{2,6},{3,7},{4,8},{5,9},{6,10},{7,11},{8,12},{9,13},{1... | collective-permute-start | bytes 884744
  222.6 0.7 copy-start.1
  230.7 7.6 %all-to-all-start.1 = ((bf16[2,3,4,6144]{3,2,1,0:T(4,128)(2,1)}), bf16[2,3,4,6144]{3,2,1,0:T(4,128)(2,1)S(1)}, u32[]{:S(2)}, u32[]{:S(2)}) async-start(bf16[2,3,4,6144]{3,2,1,0:T(4,128)(2,1)} %reshape.57), calls=%async_computation.1 | async-start | bytes 589824 | tf_op jit(solution)/shard_map/all_to_all | solution.py:49
Sparse Core Ops, SparseCore 0:
  18.6 53.1 all-gather.1
where the time goes:
time: 247 us
  waiting for transfers between devices  79.9 us (32%)
  blocking collectives  78.1 us (32%)
  matrix products  42.6 us (17%)
  starting transfers between devices  16.1 us (7%)
  local copies, waits for them, and re-layouts  15.3 us (6%)
  between operations  14.2 us (6%)
    unnamed x1, blocking collectives  69.9 us
    all_gather x1, waiting for transfers between devices, body(): piece = lax.all_gather(regrouped, 'tensor', axis=1, tiled=True)  53.3 us
    unnamed x5, waiting for transfers between devices  22.6 us
    dot_general x1, matrix products, body(): jnp.einsum('erd,edf->erf', piece, w_up, preferred_element_type=jnp.float32)  15 us
    dot_general x1, matrix products, body(): jnp.einsum('erd,edf->erf', piece, w_gate, preferred_element_type=jnp.floa...  14 us
    unnamed x4, starting transfers between devices  12.7 us
    dot_general x1, matrix products, body(): jnp.einsum('erf,efd->red', piece, w_down, preferred_element_type=jnp.floa...  12.5 us
    unnamed x13, local copies, waits for them, and re-layouts  8.41 us
  transfers between devices with their start and end apart: 6, of which 3 were waited for; matrix products, arithmetic and copies ran while one was open for 0% of the time, Pallas kernels for 0%

commit v1 on v0

--- a/solution.py
+++ b/solution.py
@@ -6,6 +6,18 @@
 EXPERTS = 8
 TOPK = 2
 CAP = 3
+
+
+def _process_joints(raw, join_dim, a_name):
+    return jnp.concatenate(
+        jax.lax.all_to_all(
+            jnp.stack([raw for _ in range(jax.lax.axis_size(a_name))], axis=0),
+            concat_axis=0,
+            split_axis=0,
+            axis_name=a_name,
+        ),
+        axis=join_dim,
+    )
 
 
 def route_places(ids):
@@ -31,7 +43,7 @@
     arrived = lax.all_to_all(buffer, "expert", split_axis=0, concat_axis=0, tiled=True)
     regrouped = arrived.reshape(n_groups, local_experts, CAP, width).transpose(1, 0, 2, 3)
     regrouped = regrouped.reshape(local_experts, n_groups * CAP, width)
-    piece = lax.all_gather(regrouped, "tensor", axis=1, tiled=True)
+    piece = _process_joints(regrouped, 1, "tensor")
     gate_act = jnp.einsum("erd,edf->erf", piece, w_gate, preferred_element_type=jnp.float32)
     up_act = jnp.einsum("erd,edf->erf", piece, w_up, preferred_element_type=jnp.float32)
     hidden = (jax.nn.silu(gate_act) * up_act).astype(jnp.bfloat16)

time: 247 us -> 290 us (1.17)
  blocking collectives: 78.1 us -> 188 us
  waiting for transfers between devices: 79.9 us -> 26.4 us
  between operations: 14.2 us -> 0.82 us
    all_to_all x0 -> x1, blocking collectives: none -> 109 us  [_process_joints(): jax.lax.all_to_all(jnp.stack([raw for _ in range(jax.lax.axis_size(a_name...]
    all_gather x1 -> x0, waiting for transfers between devices: 53.3 us -> none  [body(): piece = lax.all_gather(regrouped, 'tensor', axis=1, tiled=True)]
    unnamed x5 -> x4, waiting for transfers between devices: 22.6 us -> 22.4 us
    unnamed x13 -> x11, local copies, waits for them, and re-layouts: 8.41 us -> 8.4 us
  transfers between devices with their start and end apart: 6 -> 5, of which waited for: 3 -> 2; matrix products, arithmetic and copies ran while one was open for 0% -> 0% of each run, Pallas kernels for 0% -> 0%
where the time goes in v1:
time: 290 us; the launch traced here: 289 us
  blocking collectives  188 us (65%)
  matrix products  40.4 us (14%)
  waiting for transfers between devices  26.4 us (9%)
  local copies, waits for them, and re-layouts  16.9 us (6%)
  starting transfers between devices  16.3 us (6%)
    all_to_all x1, blocking collectives, _process_joints(): jax.lax.all_to_all(jnp.stack([raw for _ in range(jax.lax.axis_size(a_name...  109 us
    unnamed x1, blocking collectives  70.5 us
    unnamed x4, waiting for transfers between devices  22.4 us
    dot_general x1, matrix products, body(): jnp.einsum('erd,edf->erf', piece, w_up, preferred_element_type=jnp.float32)  15 us
    unnamed x4, starting transfers between devices  12.8 us
    dot_general x1, matrix products, body(): jnp.einsum('erf,efd->red', piece, w_down, preferred_element_type=jnp.floa...  12.5 us
    dot_general x1, matrix products, body(): jnp.einsum('erd,edf->erf', piece, w_gate, preferred_element_type=jnp.floa...  11.8 us
    unnamed x11, local copies, waits for them, and re-layouts  8.4 us
  transfers between devices with their start and end apart: 5, of which 2 were waited for; matrix products, arithmetic and copies ran while one was open for 0% of the time, Pallas kernels for 0%

profile of v1, /device:TPU:19, one launch (start us, length us, event | category | flops | bytes accessed | tf_op | source)
XLA Modules:
  0.0 289.3 jit_solution(2380274594425487655)
XLA Ops:
  0.0 0.8 copy.27
  0.8 0.1 eq.43
  0.9 0.2 select_reduce_fusion.1
  1.1 1.0 broadcast_in_dim.2
  2.2 0.2 convolution_convert_fusion.1
  2.5 8.2 %all_to_all.15 = bf16[2,12,6144]{2,1,0:T(8,128)(2,1)S(1)} all-to-all(bf16[2,12,6144]{2,1,0:T(8,128)(2,1)S(1)} %reshape.59), channel_id=1, replica_groups=mesh['expert'=2,'tensor'=16] {'expert'}, dimensions={0} | all-to-all | bytes 589824 | tf_op jit(solution)/shard_map/all_to_all | solution.py:43
  10.7 0.3 copy.30
  11.1 0.2 copy.31
  11.2 2.3 stack.3
  13.6 109.4 %all_to_all.16 = bf16[16,4,6,6144]{3,1,2,0:T(4,128)(2,1)S(1)} all-to-all(bf16[16,4,6,6144]{3,1,2,0:T(4,128)(2,1)S(1)} %stack.3), channel_id=1, replica_groups=mesh['expert'=2,'tensor'=16] {'tensor'}, dimensions={0} | all-to-all | bytes 9437184 | tf_op jit(solution)/shard_map/all_to_all | solution.py:13
  122.9 11.8 %fusion.4 = f32[4,96,512]{2,1,0:T(8,128)S(1)} fusion(bf16[4,6144,512]{2,1,0:T(8,128)(2,1)} %param.9, bf16[4,96,6144]{2,0,1:T(4,128)(2,1)S(1)} %bitcast.22), kind=kOutput, calls=%fused_computation.6 | convolution fusion | flops 2415919104 | bytes 30670848 | tf_op jit(solution)/shard_map/erd,edf->erf/dot_general | solution.py:47
  134.8 15.0 %fusion.9 = bf16[4,96,512]{2,1,0:T(8,128)(2,1)S(1)} fusion(bf16[4,6144,512]{2,1,0:T(8,128)(2,1)} %param.10, bf16[4,96,6144]{2,0,1:T(4,128)(2,1)S(1)} %bitcast.23, f32[4,96,512]{2,1,0:T(8,128)S(1)} %fusion.4), kind=kOutput, calls=%fused_computation.9 | convolution fusion | flops 2417098752 | bytes 31064064 | tf_op jit(solution)/shard_map/erd,edf->erf/dot_general | solution.py:48
  149.7 12.5 %fusion.1 = bf16[4,12,8,6144]{3,2,1,0:T(8,128)(2,1)S(1)} fusion(bf16[4,96,512]{2,1,0:T(8,128)(2,1)S(1)} %fusion.9, bf16[4,512,6144]{2,1,0:T(8,128)(2,1)} %param.11), kind=kOutput, calls=%fused_computation.1 | convolution fusion | flops 2418278400 | bytes 30277632 | tf_op jit(solution)/shard_map/erf,efd->red/dot_general | solution.py:51
  162.2 2.7 copy.36
  164.9 70.5 %fusion = bf16[8,24576]{1,0:T(8,128)(2,1)S(1)} fusion(bf16[96,24576]{1,0:T(8,128)(2,1)} %bitcast.24), kind=kCustom, calls=%all-reduce-scatter | all-reduce-scatter fusion | flops 3145729 | bytes 5112320
  235.4 6.3 %collective-permute-start.2 = (bf16[8,24576]{1,0:T(8,128)(2,1)S(1)}, bf16[8,24576]{1,0:T(8,128)(2,1)S(1)}, u32[]{:S(2)}, u32[]{:S(2)}) collective-permute-start(bf16[8,24576]{1,0:T(8,128)(2,1)S(1)} %fusion), channel_id=1, source_target_pairs={{0,3},{1,4},{2,5},{3,6},{4,7},{5,8},{6,9},{7,10},{8,11},{9,12},{10... | collective-permute-start | bytes 1179656
  241.7 1.9 collective-permute-start.1
  243.6 2.7 collective-permute-start
  246.4 0.1 slice
  246.5 1.9 collective-permute-start.3
  248.5 0.6 dynamic-slice.4
  249.7 22.4 %collective-permute-done.3 = bf16[6,24576]{1,0:T(8,128)(2,1)S(1)} collective-permute-done((bf16[6,24576]{1,0:T(8,128)(2,1)S(1)}, bf16[6,24576]{1,0:T(8,128)(2,1)S(1)}, u32[]{:S(2)}, u32[]{:S(2)}) %collective-permute-start.3) | collective-permute-done | bytes 294944
  272.1 0.7 copy-done
  272.9 6.1 %concatenate = bf16[38,24576]{1,0:T(8,128)(2,1)S(1)} concatenate(bf16[6,24576]{1,0:T(8,128)(2,1)} %copy-done, bf16[8,24576]{1,0:T(8,128)(2,1)S(1)} %collective-permute-done.2, bf16[8,24576]{1,0:T(8,128)(2,1)S(1)} %collective-permute-done.1, bf16[8,24576]{1,0:T(8,128)(2,1)S(1)} %collective-permute-done, bf16[8,24576]{1,0:T(8,128)(2,1)S(1)} %fusion), dimensions={0} | concatenate | bytes 3735552
  279.0 0.1 constant_dynamic-slice_fusion
  279.1 1.1 reshape.63
  280.2 3.4 %all-to-all-start.2 = ((bf16[2,3,4,6144]{3,2,1,0:T(4,128)(2,1)}), bf16[2,3,4,6144]{3,2,1,0:T(4,128)(2,1)S(1)}, u32[]{:S(2)}, u32[]{:S(2)}) async-start(bf16[2,3,4,6144]{3,2,1,0:T(4,128)(2,1)} %reshape.63), calls=%async_computation.2 | async-start | bytes 589824 | tf_op jit(solution)/shard_map/all_to_all | solution.py:61
  283.7 0.1 copy.29
  283.9 4.0 %all-to-all-done.2 = bf16[2,3,4,6144]{3,2,1,0:T(4,128)(2,1)S(1)} async-done(((bf16[2,3,4,6144]{3,2,1,0:T(4,128)(2,1)}), bf16[2,3,4,6144]{3,2,1,0:T(4,128)(2,1)S(1)}, u32[]{:S(2)}, u32[]{:S(2)}) %all-to-all-start.2) | async-done | bytes 294944 | tf_op jit(solution)/shard_map/all_to_all | solution.py:61
  287.9 0.3 copy.35
  288.1 0.3 reshape.64
  288.4 0.9 convolution_convert_fusion.2
  (16 shorter events, 0.4 us)
Async XLA Ops:
  164.9 83.6 %copy-start.2 = (u32[32]{0:T(128)S(1)}, u32[32]{0:T(128)}, u32[]{:S(2)}) copy-start(u32[32]{0:T(128)} %constant.19) | copy-start | bytes 388
  164.9 118.9 %copy-start.1 = (f32[8,2]{0,1:T(2,128)S(1)}, f32[8,2]{0,1:T(2,128)}, u32[]{:S(2)}) copy-start(f32[8,2]{0,1:T(2,128)} %param.8) | copy-start | bytes 196
  235.4 36.7 %collective-permute-start.2 = (bf16[8,24576]{1,0:T(8,128)(2,1)S(1)}, bf16[8,24576]{1,0:T(8,128)(2,1)S(1)}, u32[]{:S(2)}, u32[]{:S(2)}) collective-permute-start(bf16[8,24576]{1,0:T(8,128)(2,1)S(1)} %fusion), channel_id=1, source_target_pairs={{0,3},{1,4},{2,5},{3,6},{4,7},{5,8},{6,9},{7,10},{8,11},{9,12},{10... | collective-permute-start | bytes 1179656
  241.7 30.4 %collective-permute-start.1 = (bf16[8,24576]{1,0:T(8,128)(2,1)S(1)}, bf16[8,24576]{1,0:T(8,128)(2,1)S(1)}, u32[]{:S(2)}, u32[]{:S(2)}) collective-permute-start(bf16[8,24576]{1,0:T(8,128)(2,1)S(1)} %fusion), channel_id=1, source_target_pairs={{0,2},{1,3},{2,4},{3,5},{4,6},{5,7},{6,8},{7,9},{8,10},{9,11},{10,... | collective-permute-start | bytes 1179656
  243.6 29.3 %collective-permute-start = (bf16[8,24576]{1,0:T(8,128)(2,1)S(1)}, bf16[8,24576]{1,0:T(8,128)(2,1)S(1)}, u32[]{:S(2)}, u32[]{:S(2)}) collective-permute-start(bf16[8,24576]{1,0:T(8,128)(2,1)S(1)} %fusion), channel_id=1, source_target_pairs={{0,1},{1,2},{2,3},{3,4},{4,5},{5,6},{6,7},{7,8},{8,9},{9,10},{10,1... | collective-permute-start | bytes 1179656
  246.5 25.7 %collective-permute-start.3 = (bf16[6,24576]{1,0:T(8,128)(2,1)S(1)}, bf16[6,24576]{1,0:T(8,128)(2,1)S(1)}, u32[]{:S(2)}, u32[]{:S(2)}) collective-permute-start(bf16[6,24576]{1,0:T(8,128)(2,1)S(1)} %slice), channel_id=1, source_target_pairs={{0,4},{1,5},{2,6},{3,7},{4,8},{5,9},{6,10},{7,11},{8,12},{9,13},{1... | collective-permute-start | bytes 884744
  272.1 0.7 copy-start
  280.2 7.6 %all-to-all-start.2 = ((bf16[2,3,4,6144]{3,2,1,0:T(4,128)(2,1)}), bf16[2,3,4,6144]{3,2,1,0:T(4,128)(2,1)S(1)}, u32[]{:S(2)}, u32[]{:S(2)}) async-start(bf16[2,3,4,6144]{3,2,1,0:T(4,128)(2,1)} %reshape.63), calls=%async_computation.2 | async-start | bytes 589824 | tf_op jit(solution)/shard_map/all_to_all | solution.py:61
